TPU v7x, 32 devices: a whole 2x2x4 slice. The times are simulated.
32 devices in a mesh: groups: 2 (over y), fsdp: 4 (over z), tensor: 4 (over x, core).
Axes of the slice: x: 2, y: 2, z: 4, core: 2. Of those that a mesh axis runs over, the one named last changes fastest.
Arguments:
- tokens: bfloat16 [2048, 4608], P(('groups', 'fsdp'), 'tensor'), parts along dimension 0, may hold values from -100 to 100
- norm_gain: bfloat16 [4608], P('tensor'), may hold values from 0.25 to 1.75
- w_query: bfloat16 [4608, 4096], P('fsdp', 'tensor'), may hold values from -0.5 to 0.5
- w_key: bfloat16 [4608, 2048], P('fsdp', 'tensor'), may hold values from -0.09375 to 0.09375
- w_value: bfloat16 [4608, 2048], P('fsdp', 'tensor'), may hold values from -0.09375 to 0.09375
- w_out: bfloat16 [4096, 4608], P('tensor', 'fsdp'), may hold values from -0.5 to 0.5
- post_gain: bfloat16 [4608], P('tensor'), may hold values from 0.25 to 1.75
Outputs:
- mixed: float32 [2048, 4608], P(('groups', 'fsdp'), 'tensor'), parts along dimension 0
There are 2 independent parts, one for each index of `groups`. A program takes and returns all parts, laid end to end along the dimension named above; an argument that names none is the same for every part. Nothing has to cross between parts.
All inputs are finite; a program needn't handle non-finite values.
Results may differ from a plain program's by a relative error of at most 0.0053.
Values may be sent and summed in bfloat16 or wider, within the bound.
A program may use at most 128 MiB of HBM per device.

v0:
```python
import jax
import jax.numpy as jnp
from jax import lax
from jax.sharding import PartitionSpec as P

D = 4608
HEAD_DIM = 128
eps_norm = 1e-06
soft_cap = 50.0
attn_scale = 144.0 ** (-0.5)
rope_base = 10000.0


def rotate(values, position):
    head_dim = values.shape[-1]
    half = head_dim // 2
    freq = rope_base ** (-(jnp.arange(half, dtype=jnp.float32) * 2.0 / head_dim))
    angle = position.astype(jnp.float32)[:, None] * freq[None, :]
    cosine = jnp.cos(angle)[:, None, :]
    sine = jnp.sin(angle)[:, None, :]
    first = values[..., :half]
    second = values[..., half:]
    return jnp.concatenate(
        [first * cosine - second * sine, second * cosine + first * sine], axis=-1
    )


def attend(query, keys, values, position):
    count, heads, head_dim = query.shape
    kv_count = keys.shape[1]
    grouped = query.reshape(count, kv_count, heads // kv_count, head_dim)
    scores = (
        jnp.einsum("nkgd,mkd->kgnm", grouped, keys, preferred_element_type=jnp.float32) * attn_scale
    )
    capped = soft_cap * jnp.tanh(scores / soft_cap)
    allowed = position[None, :] <= position[:, None]
    weights = jnp.where(allowed, jnp.exp(capped), 0.0)
    probs = (weights / jnp.sum(weights, axis=-1, keepdims=True)).astype(jnp.bfloat16)
    mixed = jnp.einsum("kgnm,mkd->nkgd", probs, values, preferred_element_type=jnp.float32)
    return mixed.reshape(count, heads * head_dim).astype(jnp.bfloat16)


def on_device(tokens, norm_gain, w_query, w_key, w_value, w_out, post_gain):
    rows = tokens.shape[0]
    full_tokens, full_gain = (
        lax.all_gather(tokens, "tensor", axis=1, tiled=True),
        lax.all_gather(norm_gain, "tensor", axis=0, tiled=True),
    )
    widened = full_tokens.astype(jnp.float32)
    total = jnp.sum(widened * widened, axis=1)
    whole = (
        widened * lax.rsqrt(total / D + eps_norm)[:, None] * full_gain.astype(jnp.float32)
    ).astype(jnp.bfloat16)
    pieces = (
        lax.all_gather(w_query, "fsdp", axis=0, tiled=True),
        lax.all_gather(w_key, "fsdp", axis=0, tiled=True),
        lax.all_gather(w_value, "fsdp", axis=0, tiled=True),
    )
    query_raw, key_raw, value_raw = tuple(
        (jnp.dot(whole, piece, preferred_element_type=jnp.float32) for piece in pieces)
    )
    position = jnp.arange(rows, dtype=jnp.int32)
    local_heads = w_query.shape[1] // HEAD_DIM
    local_kv = w_key.shape[1] // HEAD_DIM
    query = rotate(query_raw.reshape(rows, local_heads, HEAD_DIM), position).astype(jnp.bfloat16)
    key = rotate(key_raw.reshape(rows, local_kv, HEAD_DIM), position).astype(jnp.bfloat16)
    value = value_raw.astype(jnp.bfloat16).reshape(rows, local_kv, HEAD_DIM)
    attn = attend(query, key, value, position)
    partial_value = jnp.dot(
        attn, lax.all_gather(w_out, "fsdp", axis=1, tiled=True), preferred_element_type=jnp.float32
    )
    proj = lax.psum_scatter(
        partial_value.astype(jnp.bfloat16), "tensor", scatter_dimension=1, tiled=True
    ).astype(jnp.float32)
    post_total = lax.psum(jnp.sum(proj * proj, axis=1), "tensor")
    branch = proj * lax.rsqrt(post_total / D + eps_norm)[:, None] * post_gain.astype(jnp.float32)
    return tokens.astype(jnp.float32) + branch


def solution(mesh):
    placed = (
        P(("groups", "fsdp"), "tensor"),
        P("tensor"),
        P("fsdp", "tensor"),
        P("fsdp", "tensor"),
        P("fsdp", "tensor"),
        P("tensor", "fsdp"),
        P("tensor"),
    )
    return jax.shard_map(
        on_device,
        mesh=mesh,
        in_specs=placed,
        out_specs=P(("groups", "fsdp"), "tensor"),
        check_vma=False,
    )
```

profile of v0, /device:TPU:0, one launch (start us, length us, event | category | flops | bytes accessed | tf_op | source)
XLA Modules:
  0.0 604.8 jit_solution(8890563282905837423)
XLA Ops:
  6.5 0.7 all-gather.7.cloned.1.call-update
  7.3 0.7 all-gather.9.cloned.1.call-update
  8.1 0.7 all-gather.11.cloned.1.call-update
  9.4 0.5 all-gather.15.cloned.1.call-update
  10.0 6.2 %all-gather = bf16[4,1,1152]{2,1,0:T(2,128)(2,1)S(1)} all-gather(bf16[1,1,1152]{2,1,0:T(2,128)(2,1)S(1)} %reshape.85), channel_id=1, replica_groups=mesh['groups'=2,'fsdp'=4,'tensor'=4] {'tensor'}, dimensions={0}, use_global_device_ids=true | all-gather | bytes 11520 | tf_op jit(solution)/shard_map/all_gather | solution.py:47
  16.9 18.8 %all-gather.7.cloned.1.call-done = bf16[256,4608]{1,0:T(8,128)(2,1)} async-done(((bf16[256,1152]{1,0:T(8,128)(2,1)}), bf16[256,4608]{1,0:T(8,128)(2,1)}) %all-gather.7.cloned.1.call-update) | async-done | bytes 2359312 | tf_op jit(solution)/shard_map/all_gather | solution.py:46
  35.7 2.4 fusion
  38.1 88.6 %all-gather.9.cloned.1.call-done = bf16[4608,512]{1,0:T(8,128)(2,1)} async-done(((bf16[1152,512]{1,0:T(8,128)(2,1)}), bf16[4608,512]{1,0:T(8,128)(2,1)}) %all-gather.9.cloned.1.call-update) | async-done | bytes 4718608 | tf_op jit(solution)/shard_map/all_gather | solution.py:57
  126.7 3.8 convolution_convert_fusion.2
  130.6 85.4 %all-gather.11.cloned.1.call-done = bf16[4608,512]{1,0:T(8,128)(2,1)} async-done(((bf16[1152,512]{1,0:T(8,128)(2,1)}), bf16[4608,512]{1,0:T(8,128)(2,1)}) %all-gather.11.cloned.1.call-update) | async-done | bytes 4718608 | tf_op jit(solution)/shard_map/all_gather | solution.py:56
  216.1 4.6 fusion.15
  220.7 1.2 reshape.83
  222.4 160.3 %all-gather.13.cloned.1.call-done = bf16[4608,1024]{1,0:T(8,128)(2,1)} async-done(((bf16[1152,1024]{1,0:T(8,128)(2,1)}), bf16[4608,1024]{1,0:T(8,128)(2,1)}) %all-gather.13.cloned.1.call-update) | async-done | bytes 9437200 | tf_op jit(solution)/shard_map/all_gather | solution.py:55
  382.7 5.3 convolution_bitcast_fusion
  388.9 2.3 bitcast_select_fusion
  391.2 3.2 convolution_convert_fusion.1
  394.4 154.7 %all-gather.15.cloned.1.call-done = bf16[1024,4608]{1,0:T(8,128)(2,1)} async-done(((bf16[1024,1152]{1,0:T(8,128)(2,1)}), bf16[1024,4608]{1,0:T(8,128)(2,1)}) %all-gather.15.cloned.1.call-update) | async-done | bytes 9437200 | tf_op jit(solution)/shard_map/all_gather | solution.py:70
  549.1 6.6 %convolution_convert_fusion = bf16[256,4608]{1,0:T(8,128)(2,1)S(1)} fusion(bf16[256,1024]{0,1:T(8,128)(2,1)S(1)} %bitcast.31, bf16[1024,4608]{1,0:T(8,128)(2,1)} %all-gather.15.cloned.1.call-done), kind=kOutput, calls=%fused_computation | convolution fusion | flops 2417098752 | bytes 12320768 | tf_op jit(solution)/shard_map/dot_general | solution.py:69
  555.7 2.4 copy.24
  558.2 0.7 copy-done.2
  558.8 30.5 %reduce-scatter.4.cloned.1.call-done = bf16[1152,256]{1,0:T(8,128)(2,1)} async-done(((bf16[4608,256]{1,0:T(8,128)(2,1)}), bf16[1152,256]{1,0:T(8,128)(2,1)}) %reduce-scatter.4.cloned.1.call-update) | async-done | bytes 589840
  589.4 1.4 copy.25
  590.9 5.8 psum.7
  596.7 1.3 fusion.5
  (33 shorter events, 3.1 us)
Async XLA Ops:
  6.5 29.2 %all-gather.7.cloned.1.call-start = ((), (), s32[]{:S(2)}) async-start(), calls=%async_computation.1 | async-start | bytes 2949120 | tf_op jit(solution)/shard_map/all_gather | solution.py:46
  7.3 119.4 %all-gather.9.cloned.1.call-start = ((), (), s32[]{:S(2)}) async-start(), calls=%async_computation.2 | async-start | bytes 5898240 | tf_op jit(solution)/shard_map/all_gather | solution.py:57
  8.0 208.1 %all-gather.11.cloned.1.call-start = ((), (), s32[]{:S(2)}) async-start(), calls=%async_computation.3 | async-start | bytes 5898240 | tf_op jit(solution)/shard_map/all_gather | solution.py:56
  8.7 1.2 copy-start.3
  8.8 374.0 %all-gather.13.cloned.1.call-start = ((), (), s32[]{:S(2)}) async-start(), calls=%async_computation.4 | async-start | bytes 11796480 | tf_op jit(solution)/shard_map/all_gather | solution.py:55
  9.3 539.8 %all-gather.15.cloned.1.call-start = ((), (), s32[]{:S(2)}) async-start(), calls=%async_computation.5 | async-start | bytes 11796480 | tf_op jit(solution)/shard_map/all_gather | solution.py:70
  9.9 579.4 %reduce-scatter.4.cloned.1.call-start = ((), (), s32[]{:S(2)}) async-start(), calls=%async_computation.6 | async-start | bytes 2949120
  35.7 91.0 %copy-start = (bf16[256,4608]{1,0:T(8,128)(2,1)S(1)}, bf16[256,4608]{1,0:T(8,128)(2,1)}, u32[]{:S(2)}) copy-start(bf16[256,4608]{1,0:T(8,128)(2,1)} %all-gather.7.cloned.1.call-done) | copy-start | bytes 7077892
  558.1 0.7 copy-start.2
  558.2 38.5 %copy-start.1 = (bf16[256,1152]{1,0:T(8,128)(2,1)S(1)}, bf16[256,1152]{1,0:T(8,128)(2,1)}, u32[]{:S(2)}) copy-start(bf16[256,1152]{1,0:T(8,128)(2,1)} %param.7) | copy-start | bytes 1769476
Sparse Core Ops, SparseCore 0:
  8.9 26.7 all-gather.6
  37.3 89.3 all-gather.8
  128.2 87.7 all-gather.10
  217.5 165.1 all-gather.12
  384.1 164.9 all-gather.14
  558.3 31.0 reduce-scatter.3
where the time goes:
time: 605 us
  waiting for transfers between devices  542 us (90%)
  matrix products  25.8 us (4%)
  between operations  13.6 us (2%)
  blocking collectives  12 us (2%)
  local copies, waits for them, and re-layouts  6.52 us (1%)
    all_gather x1, waiting for transfers between devices, on_device(): lax.all_gather(w_query, 'fsdp', axis=0, tiled=True)  160 us
    all_gather x1, waiting for transfers between devices, on_device(): lax.all_gather(w_out, 'fsdp', axis=1, tiled=True)  155 us
    all_gather x1, waiting for transfers between devices, on_device(): lax.all_gather(w_value, 'fsdp', axis=0, tiled=True)  88.6 us
    all_gather x1, waiting for transfers between devices, on_device(): lax.all_gather(w_key, 'fsdp', axis=0, tiled=True)  85.4 us
    unnamed x7, waiting for transfers between devices  33.7 us
    all_gather x1, waiting for transfers between devices, on_device(): lax.all_gather(tokens, 'tensor', axis=1, tiled=True)  18.8 us
    dot_general x3, matrix products, on_device(): jnp.dot(whole, piece, preferred_element_type=jnp.float32)  13.7 us
  transfers between devices with their start and end apart: 6, of which 6 were waited for; matrix products, arithmetic and copies ran while one was open for 4% of the time, Pallas kernels for 0%

commit v1 on v0

--- a/solution.py
+++ b/solution.py
@@ -67,7 +67,9 @@
     value = value_raw.astype(jnp.bfloat16).reshape(rows, local_kv, HEAD_DIM)
     attn = attend(query, key, value, position)
     partial_value = jnp.dot(
-        attn, lax.all_gather(w_out, "fsdp", axis=1, tiled=True), preferred_element_type=jnp.float32
+        attn,
+        jnp.concatenate(lax.all_gather(w_out, "fsdp"), axis=1),
+        preferred_element_type=jnp.float32,
     )
     proj = lax.psum_scatter(
         partial_value.astype(jnp.bfloat16), "tensor", scatter_dimension=1, tiled=True

time: 605 us -> 627 us (1.036)
  local copies, waits for them, and re-layouts: 6.52 us -> 20.1 us
    reshape x0 -> x1, local copies, waits for them, and re-layouts: none -> 12.7 us  [on_device(): jnp.concatenate(lax.all_gather(w_out, 'fsdp'), axis=1)]
  transfers between devices with their start and end apart: 6 -> 6, of which waited for: 6 -> 6; matrix products, arithmetic and copies ran while one was open for 4% -> 3% of each run, Pallas kernels for 0% -> 0%
where the time goes in v1:
time: 627 us; the launch traced here: 626 us
  waiting for transfers between devices  546 us (87%)
  matrix products  29.5 us (5%)
  local copies, waits for them, and re-layouts  20.1 us (3%)
  between operations  13.6 us (2%)
  blocking collectives  12 us (2%)
    all_gather x1, waiting for transfers between devices, on_device(): lax.all_gather(w_query, 'fsdp', axis=0, tiled=True)  161 us
    all_gather x1, waiting for transfers between devices, on_device(): lax.all_gather(w_out, 'fsdp')  160 us
    all_gather x1, waiting for transfers between devices, on_device(): lax.all_gather(w_key, 'fsdp', axis=0, tiled=True)  88.6 us
    all_gather x1, waiting for transfers between devices, on_device(): lax.all_gather(w_value, 'fsdp', axis=0, tiled=True)  83.6 us
    unnamed x7, waiting for transfers between devices  33.6 us
    all_gather x1, waiting for transfers between devices, on_device(): lax.all_gather(tokens, 'tensor', axis=1, tiled=True)  18.8 us
    dot_general x3, matrix products, on_device(): jnp.dot(whole, piece, preferred_element_type=jnp.float32)  14.2 us
    reshape x1, local copies, waits for them, and re-layouts, on_device(): jnp.concatenate(lax.all_gather(w_out, 'fsdp'), axis=1)  12.7 us
  transfers between devices with their start and end apart: 6, of which 6 were waited for; matrix products, arithmetic and copies ran while one was open for 3% of the time, Pallas kernels for 0%

profile of v1, /device:TPU:0, one launch (start us, length us, event | category | flops | bytes accessed | tf_op | source)
XLA Modules:
  0.0 626.1 jit_solution(5393370198647827783)
XLA Ops:
  6.5 0.7 all-gather.8.cloned.1.call-update
  7.3 0.7 all-gather.12.cloned.1.call-update
  8.1 0.7 all-gather.10.cloned.1.call-update
  10.0 6.2 all-gather.1
  16.9 18.8 %all-gather.8.cloned.1.call-done = bf16[256,4608]{1,0:T(8,128)(2,1)} async-done(((bf16[256,1152]{1,0:T(8,128)(2,1)}), bf16[256,4608]{1,0:T(8,128)(2,1)}) %all-gather.8.cloned.1.call-update) | async-done | bytes 2359312 | tf_op jit(solution)/shard_map/all_gather | solution.py:46
  35.7 2.4 fusion
  38.1 88.6 %all-gather.12.cloned.1.call-done = bf16[4608,512]{1,0:T(8,128)(2,1)} async-done(((bf16[1152,512]{1,0:T(8,128)(2,1)}), bf16[4608,512]{1,0:T(8,128)(2,1)}) %all-gather.12.cloned.1.call-update) | async-done | bytes 4718608 | tf_op jit(solution)/shard_map/all_gather | solution.py:56
  126.7 4.6 fusion.15
  131.2 1.2 reshape.89
  132.4 83.6 %all-gather.10.cloned.1.call-done = bf16[4608,512]{1,0:T(8,128)(2,1)} async-done(((bf16[1152,512]{1,0:T(8,128)(2,1)}), bf16[4608,512]{1,0:T(8,128)(2,1)}) %all-gather.10.cloned.1.call-update) | async-done | bytes 4718608 | tf_op jit(solution)/shard_map/all_gather | solution.py:57
  216.1 4.5 convolution_convert_fusion.2
  220.6 1.1 copy.37
  222.1 160.6 %all-gather.14.cloned.1.call-done = bf16[4608,1024]{1,0:T(8,128)(2,1)} async-done(((bf16[1152,1024]{1,0:T(8,128)(2,1)}), bf16[4608,1024]{1,0:T(8,128)(2,1)}) %all-gather.14.cloned.1.call-update) | async-done | bytes 9437200 | tf_op jit(solution)/shard_map/all_gather | solution.py:55
  382.7 5.2 convolution_bitcast_fusion
  388.8 160.3 %all-gather.16.cloned.1.call-done = bf16[4096,1152]{1,0:T(8,128)(2,1)} async-done(((bf16[1024,1152]{1,0:T(8,128)(2,1)}), bf16[4096,1152]{1,0:T(8,128)(2,1)}) %all-gather.16.cloned.1.call-update) | async-done | bytes 9437200 | tf_op jit(solution)/shard_map/all_gather | solution.py:71
  549.1 12.7 %copy.33 = bf16[1024,4,1152]{0,2,1:T(8,128)(2,1)} copy(bf16[1024,4,1152]{2,0,1:T(8,128)(2,1)} %bitcast.33) | data formatting | bytes 18874368 | tf_op jit(solution)/shard_map/reshape | solution.py:71
  561.8 2.3 bitcast_select_fusion
  564.1 2.7 convolution_convert_fusion.1
  566.8 10.2 %convolution_convert_fusion = bf16[256,4608]{1,0:T(8,128)(2,1)S(1)} fusion(bf16[256,1024]{0,1:T(8,128)(2,1)S(1)} %bitcast.41, bf16[1024,4608]{0,1:T(8,128)(2,1)} %bitcast.34), kind=kOutput, calls=%fused_computation | convolution fusion | flops 2417098752 | bytes 12320768 | tf_op jit(solution)/shard_map/dot_general | solution.py:69
  577.0 2.4 copy.38
  580.1 30.5 %reduce-scatter.4.cloned.1.call-done = bf16[1152,256]{1,0:T(8,128)(2,1)} async-done(((bf16[4608,256]{1,0:T(8,128)(2,1)}), bf16[1152,256]{1,0:T(8,128)(2,1)}) %reduce-scatter.4.cloned.1.call-update) | async-done | bytes 589840
  610.6 1.4 copy.39
  612.2 5.8 psum.7
  617.9 1.3 fusion.5
  (34 shorter events, 4.1 us)
Async XLA Ops:
  6.5 29.2 %all-gather.8.cloned.1.call-start = ((), (), s32[]{:S(2)}) async-start(), calls=%async_computation.1 | async-start | bytes 2949120 | tf_op jit(solution)/shard_map/all_gather | solution.py:46
  7.3 119.4 %all-gather.12.cloned.1.call-start = ((), (), s32[]{:S(2)}) async-start(), calls=%async_computation.3 | async-start | bytes 5898240 | tf_op jit(solution)/shard_map/all_gather | solution.py:56
  8.0 208.1 %all-gather.10.cloned.1.call-start = ((), (), s32[]{:S(2)}) async-start(), calls=%async_computation.2 | async-start | bytes 5898240 | tf_op jit(solution)/shard_map/all_gather | solution.py:57
  8.7 1.2 copy-start.3
  8.8 374.0 %all-gather.14.cloned.1.call-start = ((), (), s32[]{:S(2)}) async-start(), calls=%async_computation.4 | async-start | bytes 11796480 | tf_op jit(solution)/shard_map/all_gather | solution.py:55
  9.3 539.8 %all-gather.16.cloned.1.call-start = ((), (), s32[]{:S(2)}) async-start(), calls=%async_computation.5 | async-start | bytes 11796480 | tf_op jit(solution)/shard_map/all_gather | solution.py:71
  9.9 600.7 %reduce-scatter.4.cloned.1.call-start = ((), (), s32[]{:S(2)}) async-start(), calls=%async_computation.6 | async-start | bytes 2949120
  35.7 91.0 %copy-start = (bf16[256,4608]{1,0:T(8,128)(2,1)S(1)}, bf16[256,4608]{1,0:T(8,128)(2,1)}, u32[]{:S(2)}) copy-start(bf16[256,4608]{1,0:T(8,128)(2,1)} %all-gather.8.cloned.1.call-done) | copy-start | bytes 7077892
  579.5 0.7 copy-start.2
  579.5 38.5 %copy-start.1 = (bf16[256,1152]{1,0:T(8,128)(2,1)S(1)}, bf16[256,1152]{1,0:T(8,128)(2,1)}, u32[]{:S(2)}) copy-start(bf16[256,1152]{1,0:T(8,128)(2,1)} %param.7) | copy-start | bytes 1769476
Sparse Core Ops, SparseCore 0:
  8.9 26.7 all-gather.7
  37.3 89.3 all-gather.11
  128.2 87.7 all-gather.9
  217.5 165.1 all-gather.13
  384.1 164.9 all-gather.15
  579.6 30.9 reduce-scatter.3
